TPU v7x, 32 devices: a whole 2x2x4 slice. The times are simulated.
32 devices in a mesh: node: 16 (over z, y, core), harm: 2 (over x).
Axes of the slice: x: 2, y: 2, z: 4, core: 2. Of those that a mesh axis runs over, the one named last changes fastest.
Arguments:
- spectrum: float32 [128, 3, 98304], P('harm', None, 'node'), may hold values from -2 to 2
- source: float32 [128, 3, 98304], P('harm', None, 'node'), may hold values from -4 to 4
- coupling: bfloat16 [768, 4, 128, 128], P('node'), may hold values from -0.75 to 0.75
- capacitance: float32 [98304], P('node'), may hold values from 0.5 to 4
- saturation: float32 [98304], P('node'), may hold values from 0.1 to 1
- steepness: float32 [98304], P('node'), may hold values from 0.5 to 4
- junction: float32 [98304], P('node'), may hold values from 0.2 to 2
- halo_list: int32 [16, 4, 4], replicated, may hold values from 0 to 47, as said below
- neighbour_slot: int32 [768, 4], P('node'), may hold values from 0 to 64, as said below
Outputs:
- residual: float32 [128, 3, 98304], P('harm', None, 'node')
Inputs may be any that keep to these rules, and one draw needn't show every extreme that they name: `halo_list`: row [m, j] lists 4 distinct blocks of device m, by index among its 48 blocks, needed by the device at index m + o_j along node, o = (-2, -1, 1, 2). `neighbour_slot`: column 0 of block b is b's own index among the 48 blocks of its device d. Other entries v: own block v if v < 48; block halo_list[m, j, s] of device m = d - o_j if v = 48 + j * 4 + s, only where m lies on the mesh; v = 64 is an empty entry. Every such slot of a device whose sender lies on the mesh is named by some entry of the device.
All inputs are finite; a program needn't handle non-finite values.
Results may differ from a plain program's by a relative error of at most 0.0025.
Values may be sent and summed in bfloat16 or wider, within the bound.
A program may use at most 128 MiB of HBM per device.

v0:
```python
import functools

import jax
import jax.numpy as jnp
import numpy as np
from jax import lax
from jax.experimental import pallas as pl
from jax.experimental.pallas import tpu as pltpu
from jax.sharding import PartitionSpec as P

LOG_TWO = 0.6931471805599453
OFFSETS = (-2, -1, 1, 2)
LANES = 128
BOUNDS = (0, 4, 12, 20, 28, 36, 44, 48)
EARLY = 3
VMEM_BYTES = 60 << 20


def fourier_tables(length):
    sample = np.arange(length)[:, None]
    column = np.arange(length)[None, :]
    angle = 2.0 * np.pi / length * (column // 2 * sample % length)
    table = np.where(column % 2 == 1, np.sin(angle), np.cos(angle))
    table = np.where(column == 1, np.where(sample % 2 == 0, 1.0, -1.0), table)
    weights = np.where(np.arange(length) < 2, 1.0, 2.0) / length
    analysis = table.T * weights[:, None]
    pulsation = np.arange(length // 2)[:, None, None] / (length // 2)
    pairs = analysis.reshape(length // 2, 2, length)
    slope = np.concatenate([pulsation * pairs[:, 1:], -pulsation * pairs[:, :1]], axis=1)
    return table, analysis, slope.reshape(length, length)


def split(table):
    high = table.astype(jnp.bfloat16)
    low = (table - high.astype(jnp.float32)).astype(jnp.bfloat16)
    return high, low


def round_kernel(x_ref, out_ref):
    out_ref[...] = x_ref[...].astype(jnp.bfloat16)


def halo_kernel(list_ref, x_ref, *out_refs):
    slots = list_ref.shape[0] // len(out_refs)
    for direction, out_ref in enumerate(out_refs):
        for slot in range(slots):
            start = pl.multiple_of(list_ref[direction * slots + slot] * LANES, LANES)
            out_ref[:, :, slot * LANES : (slot + 1) * LANES] = x_ref[
                :, :, pl.ds(start, LANES)
            ].astype(jnp.bfloat16)


def coupling_kernel(per_step, early_steps, slot_ref, x_ref, *refs):
    halo_refs = refs[: len(OFFSETS)]
    coupling_ref, source_ref, capacitance_ref, pulsation_ref, before_ref, out_ref, pool_ref = refs[
        len(OFFSETS) :
    ]
    points, rows, nodes = x_ref.shape
    own = nodes // LANES
    count = coupling_ref.shape[1]
    step = pl.program_id(0)

    @pl.when(step == 0)
    def _():
        for block in range(own):
            part = x_ref[:, :, block * LANES : (block + 1) * LANES].astype(jnp.bfloat16)
            pool_ref[block] = part.reshape(points * rows, LANES)
        place = own
        for halo_ref in halo_refs:
            for slot in range(halo_ref.shape[2] // LANES):
                part = halo_ref[:, :, slot * LANES : (slot + 1) * LANES]
                pool_ref[place] = part.reshape(points * rows, LANES)
                place += 1
        pool_ref[place] = jnp.zeros((points * rows, LANES), jnp.bfloat16)

    pulsation = pulsation_ref[...]
    even = lax.broadcasted_iota(jnp.int32, (rows, LANES), 0) % 2 == 0
    for inner in range(per_step):
        block = step * per_step + inner
        picked = [pool_ref[slot_ref[block * count + k]] for k in range(count)]
        gathered = jnp.concatenate(picked, axis=1)
        matrix = jnp.concatenate([coupling_ref[inner, k] for k in range(count)], axis=1)
        coupled = lax.dot_general(
            gathered, matrix, (((1,), (1,)), ((), ())), preferred_element_type=jnp.float32
        )
        lanes = pl.ds(inner * LANES, LANES)
        columns = pl.ds(pl.multiple_of(block * LANES, LANES), LANES)
        scaled = pulsation * capacitance_ref[:, lanes]
        for point in range(points):
            values = x_ref[point, :, columns]
            other = jnp.where(
                even, pltpu.roll(values, rows - 1, 0), pltpu.roll(values, 1, 0)
            )
            before = jnp.where(step < early_steps, before_ref[point, :, lanes], 0.0)
            out_ref[point, :, lanes] = (
                before
                + coupled[point * rows : (point + 1) * rows]
                + scaled * other
                - source_ref[point, :, lanes]
            )


def nonlinear_kernel(shares, adds, synthesis_ref, analysis_ref, *refs):
    spectra = refs[:shares]
    saturation_ref, steepness_ref, junction_ref, *partial_ref, out_ref = refs[shares:]
    saturation = saturation_ref[...]
    steepness = steepness_ref[...]
    junction = junction_ref[...]
    synthesis = synthesis_ref[...]
    analysis = analysis_ref[...]
    for point in range(out_ref.shape[0]):
        columns = [ref[point] for ref in spectra]
        stacked = jnp.concatenate(columns + columns, axis=0)
        voltage = jnp.dot(synthesis, stacked, preferred_element_type=jnp.float32)
        drive = steepness * voltage
        softplus = jnp.maximum(drive, 0.0) + jnp.log(1.0 + jnp.exp(-jnp.abs(drive)))
        current = (saturation * (softplus - LOG_TWO)).astype(jnp.bfloat16)
        charge = (junction * voltage * lax.rsqrt(1.0 + voltage * voltage)).astype(jnp.bfloat16)
        samples = jnp.concatenate([current, charge], axis=0)
        result = jnp.dot(analysis, samples, preferred_element_type=jnp.float32)
        out_ref[point] = result + partial_ref[0][point] if adds else result


def call(kernel, grid, in_specs, out_specs, out_shape, flops, moved, **rest):
    return pl.pallas_call(
        kernel,
        grid=grid,
        in_specs=in_specs,
        out_specs=out_specs,
        out_shape=out_shape,
        compiler_params=pltpu.CompilerParams(vmem_limit_bytes=VMEM_BYTES),
        cost_estimate=pl.CostEstimate(flops=flops, bytes_accessed=moved, transcendentals=0),
        **rest,
    )


def local(
    spectrum,
    source,
    coupling,
    capacitance,
    saturation,
    steepness,
    junction,
    halo_list,
    neighbour_slot,
):
    rows, points, nodes = spectrum.shape
    shares = lax.axis_size("harm")
    length = rows * shares
    me = lax.axis_index("harm")
    x = jnp.transpose(spectrum, (1, 0, 2))
    injected = jnp.transpose(source, (1, 0, 2))
    smem = pl.BlockSpec(memory_space=pltpu.SMEM)

    def fixed(*shape):
        return pl.BlockSpec(shape, lambda i: (0,) * len(shape))

    blocks = nodes // LANES
    bounds = [bound * blocks // BOUNDS[-1] for bound in BOUNDS]
    unit = 2 if all(bound % 2 == 0 for bound in bounds) else 1
    tile = unit * LANES
    chunk_count = len(bounds) - 1
    own_chunks, arrived = [], []
    for chunk in range(chunk_count):
        low, high = bounds[chunk] * LANES, bounds[chunk + 1] * LANES
        if chunk == 0:
            shape = (points, rows, high)
            piece = call(
                round_kernel,
                (1,),
                [fixed(*shape)],
                fixed(*shape),
                jax.ShapeDtypeStruct(shape, jnp.bfloat16),
                0,
                points * rows * high * 6,
            )(x)
        else:
            piece = x[:, :, low:high].astype(jnp.bfloat16)
        own_chunks.append(piece)
        arrived.append(
            [
                lax.ppermute(piece, "harm", [(i, (i + by) % shares) for i in range(shares)])
                for by in range(1, shares)
            ]
        )

    slots = halo_list.shape[2]
    listed = halo_list[lax.axis_index("node")].reshape(-1)
    packed = call(
        halo_kernel,
        (1,),
        [smem, fixed(points, rows, nodes)],
        [fixed(points, rows, slots * LANES) for _ in OFFSETS],
        [jax.ShapeDtypeStruct((points, rows, slots * LANES), jnp.bfloat16) for _ in OFFSETS],
        0,
        points * rows * nodes * 4,
    )(listed, x)
    devices = lax.axis_size("node")
    halos = []
    for direction, by in enumerate(OFFSETS):
        pairs = [(i, i + by) for i in range(devices) if 0 <= i + by < devices]
        halos.append(lax.ppermute(packed[direction], "node", pairs))

    synthesis, analysis, slope = (
        jnp.asarray(table, jnp.float32) for table in fourier_tables(length)
    )
    senders = [(me - by) % shares for by in range(shares)]
    synthesis = jnp.concatenate(
        [lax.dynamic_slice_in_dim(synthesis, s * rows, rows, 1) for s in senders], axis=1
    )
    synthesis = jnp.concatenate(split(synthesis), axis=1)
    analysis = jnp.concatenate(
        [lax.dynamic_slice_in_dim(table, me * rows, rows, 0) for table in (analysis, slope)],
        axis=1,
    ).astype(jnp.bfloat16)
    scales = [value.reshape(1, -1) for value in (saturation, steepness, junction)]
    result_shape = jax.ShapeDtypeStruct((points, rows, nodes), jnp.float32)

    def nonlinear(chunk, total, adds):
        first = bounds[chunk] // unit
        width = (bounds[chunk + 1] - bounds[chunk]) * LANES
        spectra = [own_chunks[chunk]] + arrived[chunk]
        here = pl.BlockSpec((points, rows, tile), lambda i: (0, 0, first + i))
        before = [] if total is None else [total]
        before_spec = here if adds else pl.BlockSpec(memory_space=pl.ANY)
        return call(
            functools.partial(nonlinear_kernel, shares, adds),
            (width // tile,),
            [fixed(*synthesis.shape), fixed(*analysis.shape)]
            + [pl.BlockSpec((points, rows, tile), lambda i: (0, 0, i)) for _ in spectra]
            + [pl.BlockSpec((1, tile), lambda i: (0, first + i))] * 3
            + [before_spec for _ in before],
            here,
            result_shape,
            8 * length * length * points * width,
            4 * points * rows * width * 3,
            input_output_aliases={5 + shares: 0} if before else {},
        )(synthesis, analysis, *spectra, *scales, *before)

    total = None
    for chunk in range(EARLY):
        total = nonlinear(chunk, total, False)

    count = neighbour_slot.shape[1]
    per_step = 4 if all(bound % 4 == 0 for bound in bounds) else 1
    step_width = per_step * LANES
    row_ids = me * rows + jnp.arange(rows, dtype=jnp.int32)
    rate = (row_ids // 2).astype(jnp.float32) / (length // 2)
    rate = jnp.where(row_ids % 2 == 0, rate, -rate)
    rate = jnp.broadcast_to(rate[:, None], (rows, LANES))
    value_spec = pl.BlockSpec((points, rows, step_width), lambda i: (0, 0, i))
    total = call(
        functools.partial(coupling_kernel, per_step, bounds[EARLY] // per_step),
        (blocks // per_step,),
        [smem, fixed(points, rows, nodes)]
        + [fixed(points, rows, slots * LANES) for _ in OFFSETS]
        + [
            pl.BlockSpec((per_step, count, LANES, LANES), lambda i: (i, 0, 0, 0)),
            value_spec,
            pl.BlockSpec((1, step_width), lambda i: (0, i)),
            fixed(rows, LANES),
            value_spec,
        ],
        value_spec,
        result_shape,
        2 * points * rows * nodes * count * LANES,
        coupling.size * 2 + 3 * x.size * 4,
        scratch_shapes=[
            pltpu.VMEM((blocks + len(OFFSETS) * slots + 1, points * rows, LANES), jnp.bfloat16)
        ],
        input_output_aliases={6 + len(OFFSETS): 0},
    )(
        neighbour_slot.reshape(-1),
        x,
        *halos,
        coupling,
        injected,
        capacitance.reshape(1, -1),
        rate,
        total,
    )
    for chunk in range(EARLY, chunk_count):
        total = nonlinear(chunk, total, True)
    return jnp.transpose(total, (1, 0, 2))


def solution(mesh):
    in_specs = (
        P("harm", None, "node"),
        P("harm", None, "node"),
        P("node", None, None, None),
        P("node"),
        P("node"),
        P("node"),
        P("node"),
        P(),
        P("node", None),
    )
    out_specs = P("harm", None, "node")
    return jax.shard_map(local, mesh=mesh, in_specs=in_specs, out_specs=out_specs, check_vma=False)
```

profile of v0, /device:TPU:1, one launch (start us, length us, event | category | flops | bytes accessed | tf_op | source)
XLA Modules:
  0.0 83.0 jit_solution(17915079343382894320)
XLA Ops:
  0.0 1.7 %shard_map.119.refs_0_ = bf16[3,64,512]{2,1,0:T(8,128)(2,1)} custom-call(f32[3,64,6144]{2,1,0:T(8,128)} %bitcast.8), custom_call_target="tpu_custom_call" | custom-call | bytes 589824 | tf_op jit(solution)/shard_map/pallas_call | solution.py:169
  1.7 2.0 %collective-permute-start.10 = (bf16[3,64,512]{2,1,0:T(8,128)(2,1)}, bf16[3,64,512]{2,1,0:T(8,128)(2,1)}, u32[]{:S(2)}, u32[]{:S(2)}) collective-permute-start(bf16[3,64,512]{2,1,0:T(8,128)(2,1)} %shard_map.119.refs_0_), channel_id=1, source_target_pairs={{0,1},{1,0},{2,3},{3,2},{4,5},{5,4},{6,7},{7,6},{8,9},{9,8},{10,11... | collective-permute-start | bytes 589832 | tf_op jit(solution)/shard_map/ppermute | solution.py:183
  3.7 2.6 %bitcast_convert_fusion = bf16[3,64,6144]{2,1,0:T(8,128)(2,1)S(1)} fusion(f32[64,3,6144]{2,0,1:T(8,128)} %param.12), kind=kLoop, calls=%fused_computation.16 | loop fusion | flops 1179648 | bytes 7077888 | tf_op jit(solution)/shard_map/convert.5
  6.4 1.0 %fusion.1 = (bf16[3,64,1024]{2,1,0:T(8,128)(2,1)}, bf16[3,64,1024]{2,1,0:T(8,128)(2,1)}, bf16[3,64,1024]{2,1,0:T(8,128)(2,1)S(1)}, bf16[3,64,1024]{2,1,0:T(8,128)(2,1)S(1)}, bf16[3,64,1024]{2,1,0:T(8,128)(2,1)S(1)}) fusion(bf16[3,64,6144]{2,1,0:T(8,128)(2,1)S(1)} %bitcast_convert_fusion), kind=kLoop, calls=%fused_computation.17 | loop fusion | bytes 3932160 | tf_op jit(solution)/shard_map/slice | solution.py:179
  7.4 1.5 %collective-permute-start.8 = (bf16[3,64,1024]{2,1,0:T(8,128)(2,1)}, bf16[3,64,1024]{2,1,0:T(8,128)(2,1)}, u32[]{:S(2)}, u32[]{:S(2)}) collective-permute-start(bf16[3,64,1024]{2,1,0:T(8,128)(2,1)} %get-tuple-element.14.refs_0_), channel_id=1, source_target_pairs={{0,1},{1,0},{2,3},{3,2},{4,5},{5,4},{6,7},{7,6},{8,9},{9,8},{10,11... | collective-permute-start | bytes 1179656 | tf_op jit(solution)/shard_map/ppermute | solution.py:183
  9.1 0.7 reshape_squeeze.3.list_ref
  9.8 3.5 %shard_map.118 = (bf16[3,64,512]{2,1,0:T(8,128)(2,1)}, bf16[3,64,512]{2,1,0:T(8,128)(2,1)}, bf16[3,64,512]{2,1,0:T(8,128)(2,1)}, bf16[3,64,512]{2,1,0:T(8,128)(2,1)}) custom-call(s32[16]{0:T(128)} %reshape_squeeze.3.list_ref, f32[3,64,6144]{2,1,0:T(8,128)} %bitcast.9), custom_call_target="tpu_custom_call" | custom-call | bytes 4718592 | tf_op jit(solution)/shard_map/pallas_call | solution.py:190
  13.2 1.3 %collective-permute-start.4 = (bf16[3,64,512]{2,1,0:T(8,128)(2,1)}, bf16[3,64,512]{2,1,0:T(8,128)(2,1)}, u32[]{:S(2)}, u32[]{:S(2)}) collective-permute-start(bf16[3,64,512]{2,1,0:T(8,128)(2,1)} %get-tuple-element.9), channel_id=1, source_target_pairs={{4,0},{6,2},{8,4},{10,6},{12,8},{14,10},{16,12},{18,14},{20,16},{2... | collective-permute-start | bytes 589832 | tf_op jit(solution)/shard_map/ppermute | solution.py:203
  14.5 3.4 %collective-permute-start.5 = (bf16[3,64,512]{2,1,0:T(8,128)(2,1)}, bf16[3,64,512]{2,1,0:T(8,128)(2,1)}, u32[]{:S(2)}, u32[]{:S(2)}) collective-permute-start(bf16[3,64,512]{2,1,0:T(8,128)(2,1)} %get-tuple-element.10), channel_id=1, source_target_pairs={{2,0},{4,2},{6,4},{8,6},{10,8},{12,10},{14,12},{16,14},{18,16},{20... | collective-permute-start | bytes 589832 | tf_op jit(solution)/shard_map/ppermute | solution.py:203
  18.0 1.0 %constant_dynamic-slice_fusion.1 = (f32[128,64]{1,0:T(8,128)S(1)}, f32[128,64]{1,0:T(8,128)S(1)}) fusion(f32[128,128]{1,0:T(8,128)} %constant.63.clone, s32[]{:T(128)S(6)} %select_n.52, s32[]{:T(128)S(6)} %select_n.54), kind=kLoop, calls=%fused_computation.12 | loop fusion | bytes 131080 | tf_op jit(solution)/shard_map/dynamic_slice | solution.py:210
  19.0 0.7 fusion
  19.7 0.7 subtract_convert_fusion
  20.4 1.4 %pad_maximum_fusion.1.synthesis_ref = bf16[128,256]{1,0:T(8,128)(2,1)} fusion(bf16[128,128]{1,0:T(8,128)(2,1)} %subtract_convert_fusion, bf16[128,128]{1,0:T(8,128)(2,1)} %fusion), kind=kLoop, calls=%fused_computation.1 | loop fusion | flops 131072 | bytes 131072 | tf_op jit(solution)/shard_map/concatenate | solution.py:212
  21.8 0.7 dynamic-slice_convert_fusion
  22.6 1.5 %collective-permute-start.2 = (bf16[3,64,1024]{2,1,0:T(8,128)(2,1)S(1)}, bf16[3,64,1024]{2,1,0:T(8,128)(2,1)}, u32[]{:S(2)}, u32[]{:S(2)}) collective-permute-start(bf16[3,64,1024]{2,1,0:T(8,128)(2,1)S(1)} %get-tuple-element.16.refs_0_), channel_id=1, source_target_pairs={{0,1},{1,0},{2,3},{3,2},{4,5},{5,4},{6,7},{7,6},{8,9},{9,8},{10,11... | collective-permute-start | bytes 1179656 | tf_op jit(solution)/shard_map/ppermute | solution.py:183
  24.0 0.6 pad_maximum_fusion.2.analysis_ref
  24.7 0.7 slice.30.refs_0_
  25.5 0.7 reshape.53.slot_ref
  26.2 4.7 %collective-permute-start.6 = (bf16[3,64,512]{2,1,0:T(8,128)(2,1)}, bf16[3,64,512]{2,1,0:T(8,128)(2,1)S(1)}, u32[]{:S(2)}, u32[]{:S(2)}) collective-permute-start(bf16[3,64,512]{2,1,0:T(8,128)(2,1)} %get-tuple-element.11), channel_id=1, source_target_pairs={{0,2},{2,4},{4,6},{6,8},{8,10},{10,12},{12,14},{14,16},{16,18},{18... | collective-permute-start | bytes 589832 | tf_op jit(solution)/shard_map/ppermute | solution.py:203
  30.9 4.1 %collective-permute-start.7 = (bf16[3,64,512]{2,1,0:T(8,128)(2,1)}, bf16[3,64,512]{2,1,0:T(8,128)(2,1)S(1)}, u32[]{:S(2)}, u32[]{:S(2)}) collective-permute-start(bf16[3,64,512]{2,1,0:T(8,128)(2,1)} %get-tuple-element.12), channel_id=1, source_target_pairs={{0,4},{2,6},{4,8},{6,10},{8,12},{10,14},{12,16},{14,18},{16,20},{1... | collective-permute-start | bytes 589832 | tf_op jit(solution)/shard_map/ppermute | solution.py:203
  35.3 2.9 %shard_map.120.refs_5_ = f32[3,64,6144]{2,1,0:T(8,128)} custom-call(bf16[128,256]{1,0:T(8,128)(2,1)} %pad_maximum_fusion.1.synthesis_ref, bf16[64,256]{1,0:T(8,128)(2,1)} %pad_maximum_fusion.2.analysis_ref, bf16[3,64,512]{2,1,0:T(8,128)(2,1)} %shard_map.119.refs_0_, bf16[3,64,512]{2,1,0:T(8,128)(2,1)} %collective-permute-done.10.refs_1_, ...), custom_call_target="tpu_custom_call" | custom-call | flops 201326592 | bytes 1179648 | tf_op jit(solution)/shard_map/pallas_call | solution.py:227
  38.2 4.6 %shard_map.121.refs_5_ = f32[3,64,6144]{2,1,0:T(8,128)} custom-call(bf16[128,256]{1,0:T(8,128)(2,1)} %pad_maximum_fusion.1.synthesis_ref, bf16[64,256]{1,0:T(8,128)(2,1)} %pad_maximum_fusion.2.analysis_ref, bf16[3,64,1024]{2,1,0:T(8,128)(2,1)} %get-tuple-element.13.refs_0_, ...), custom_call_target="tpu_custom_call", output_to_operand_aliasing={{}: (7, {})} | custom-call | flops 402653184 | bytes 2359296 | tf_op jit(solution)/shard_map/pallas_call | solution.py:227
  42.8 4.6 %shard_map.122.refs_8_ = f32[3,64,6144]{2,1,0:T(8,128)} custom-call(bf16[128,256]{1,0:T(8,128)(2,1)} %pad_maximum_fusion.1.synthesis_ref, bf16[64,256]{1,0:T(8,128)(2,1)} %pad_maximum_fusion.2.analysis_ref, bf16[3,64,1024]{2,1,0:T(8,128)(2,1)} %get-tuple-element.14.refs_0_, ...), custom_call_target="tpu_custom_call", output_to_operand_aliasing={{}: (7, {})} | custom-call | flops 402653184 | bytes 2359296 | tf_op jit(solution)/shard_map/pallas_call | solution.py:227
  47.4 1.3 %collective-permute-start = (bf16[3,64,512]{2,1,0:T(8,128)(2,1)S(1)}, bf16[3,64,512]{2,1,0:T(8,128)(2,1)S(1)}, u32[]{:S(2)}, u32[]{:S(2)}) collective-permute-start(bf16[3,64,512]{2,1,0:T(8,128)(2,1)S(1)} %copy-done.4), channel_id=1, source_target_pairs={{0,1},{1,0},{2,3},{3,2},{4,5},{5,4},{6,7},{7,6},{8,9},{9,8},{10,11... | collective-permute-start | bytes 589832 | tf_op jit(solution)/shard_map/ppermute | solution.py:183
  48.7 0.7 broadcast_in_dim.2.refs_7_
  49.4 15.0 %shard_map.123.refs_5_ = f32[3,64,6144]{2,1,0:T(8,128)} custom-call(s32[192]{0:T(256)} %reshape.53.slot_ref, f32[3,64,6144]{2,1,0:T(8,128)} %bitcast.10, bf16[3,64,512]{2,1,0:T(8,128)(2,1)} %collective-permute-done.4.refs_0_, bf16[3,64,512]{2,1,0:T(8,128)(2,1)} %collective-permute-done.5.refs_1_, ...), custom_call_target="tpu_custom_call", output_to_operand_aliasing={{}: (10, {})} | custom-call | flops 1207959552 | bytes 20447232 | tf_op jit(solution)/shard_map/pallas_call | solution.py:253
  64.4 4.7 %shard_map.124.refs_5_ = f32[3,64,6144]{2,1,0:T(8,128)} custom-call(bf16[128,256]{1,0:T(8,128)(2,1)} %pad_maximum_fusion.1.synthesis_ref, bf16[64,256]{1,0:T(8,128)(2,1)} %pad_maximum_fusion.2.analysis_ref, bf16[3,64,1024]{2,1,0:T(8,128)(2,1)} %copy-done.3, bf16[3,64,1024]{2,1,0:T(8,128)(2,1)} %collective-permute-done.3.refs_1_, ...), custom_call_target="tpu_custom_call", output_to_operand_aliasing={{}: (7, {})} | custom-call | flops 402653184 | bytes 2359296 | tf_op jit(solution)/shard_map/pallas_call | solution.py:227
  69.1 4.7 %shard_map.125.refs_5_ = f32[3,64,6144]{2,1,0:T(8,128)} custom-call(bf16[128,256]{1,0:T(8,128)(2,1)} %pad_maximum_fusion.1.synthesis_ref, bf16[64,256]{1,0:T(8,128)(2,1)} %pad_maximum_fusion.2.analysis_ref, bf16[3,64,1024]{2,1,0:T(8,128)(2,1)} %copy-done.2, bf16[3,64,1024]{2,1,0:T(8,128)(2,1)} %collective-permute-done.2.refs_1_, ...), custom_call_target="tpu_custom_call", output_to_operand_aliasing={{}: (7, {})} | custom-call | flops 402653184 | bytes 2359296 | tf_op jit(solution)/shard_map/pallas_call | solution.py:227
  73.8 0.7 copy-done.5
  74.6 4.7 %shard_map.126.refs_5_ = f32[3,64,6144]{2,1,0:T(8,128)} custom-call(bf16[128,256]{1,0:T(8,128)(2,1)} %pad_maximum_fusion.1.synthesis_ref, bf16[64,256]{1,0:T(8,128)(2,1)} %pad_maximum_fusion.2.analysis_ref, bf16[3,64,1024]{2,1,0:T(8,128)(2,1)} %copy-done.1, bf16[3,64,1024]{2,1,0:T(8,128)(2,1)} %copy-done.5, ...), custom_call_target="tpu_custom_call", output_to_operand_aliasing={{}: (7, {})} | custom-call | flops 402653184 | bytes 2359296 | tf_op jit(solution)/shard_map/pallas_call | solution.py:227
  79.3 0.7 copy-done.8
  80.0 3.0 %shard_map.127 = f32[3,64,6144]{2,1,0:T(8,128)} custom-call(bf16[128,256]{1,0:T(8,128)(2,1)} %pad_maximum_fusion.1.synthesis_ref, bf16[64,256]{1,0:T(8,128)(2,1)} %pad_maximum_fusion.2.analysis_ref, bf16[3,64,512]{2,1,0:T(8,128)(2,1)} %slice.30.refs_0_, bf16[3,64,512]{2,1,0:T(8,128)(2,1)} %copy-done.8, ...), custom_call_target="tpu_custom_call", output_to_operand_aliasing={{}: (7, {})} | custom-call | flops 201326592 | bytes 1179648 | tf_op jit(solution)/shard_map/pallas_call | solution.py:227
  (35 shorter events, 0.7 us)
Async XLA Ops:
  0.0 8.9 %copy-start = (s32[16,4,4]{0,2,1:T(4,128)S(1)}, s32[16,4,4]{0,2,1:T(4,128)}, u32[]{:S(2)}) copy-start(s32[16,4,4]{0,2,1:T(4,128)} %param.19) | copy-start | bytes 3076
  1.7 20.9 %collective-permute-start.10 = (bf16[3,64,512]{2,1,0:T(8,128)(2,1)}, bf16[3,64,512]{2,1,0:T(8,128)(2,1)}, u32[]{:S(2)}, u32[]{:S(2)}) collective-permute-start(bf16[3,64,512]{2,1,0:T(8,128)(2,1)} %shard_map.119.refs_0_), channel_id=1, source_target_pairs={{0,1},{1,0},{2,3},{3,2},{4,5},{5,4},{6,7},{7,6},{8,9},{9,8},{10,11... | collective-permute-start | bytes 589832 | tf_op jit(solution)/shard_map/ppermute | solution.py:183
  6.4 19.0 %copy-start.9 = (s32[48,4]{0,1:T(4,128)S(1)}, s32[48,4]{0,1:T(4,128)}, u32[]{:S(2)}) copy-start(s32[48,4]{0,1:T(4,128)} %param.20) | copy-start | bytes 2308
  7.4 30.8 %copy-start.1 = (bf16[3,64,1024]{2,1,0:T(8,128)(2,1)}, bf16[3,64,1024]{2,1,0:T(8,128)(2,1)S(1)}, u32[]{:S(2)}) copy-start(bf16[3,64,1024]{2,1,0:T(8,128)(2,1)S(1)} %get-tuple-element.17.refs_0_) | copy-start | bytes 1179652
  7.4 30.8 %copy-start.2 = (bf16[3,64,1024]{2,1,0:T(8,128)(2,1)}, bf16[3,64,1024]{2,1,0:T(8,128)(2,1)S(1)}, u32[]{:S(2)}) copy-start(bf16[3,64,1024]{2,1,0:T(8,128)(2,1)S(1)} %get-tuple-element.16.refs_0_) | copy-start | bytes 1179652
  7.4 30.8 %copy-start.3 = (bf16[3,64,1024]{2,1,0:T(8,128)(2,1)}, bf16[3,64,1024]{2,1,0:T(8,128)(2,1)S(1)}, u32[]{:S(2)}) copy-start(bf16[3,64,1024]{2,1,0:T(8,128)(2,1)S(1)} %get-tuple-element.15.refs_0_) | copy-start | bytes 1179652
  7.4 23.5 %collective-permute-start.9 = (bf16[3,64,1024]{2,1,0:T(8,128)(2,1)}, bf16[3,64,1024]{2,1,0:T(8,128)(2,1)}, u32[]{:S(2)}, u32[]{:S(2)}) collective-permute-start(bf16[3,64,1024]{2,1,0:T(8,128)(2,1)} %get-tuple-element.13.refs_0_), channel_id=1, source_target_pairs={{0,1},{1,0},{2,3},{3,2},{4,5},{5,4},{6,7},{7,6},{8,9},{9,8},{10,11... | collective-permute-start | bytes 1179656 | tf_op jit(solution)/shard_map/ppermute | solution.py:183
  7.4 27.5 %collective-permute-start.8 = (bf16[3,64,1024]{2,1,0:T(8,128)(2,1)}, bf16[3,64,1024]{2,1,0:T(8,128)(2,1)}, u32[]{:S(2)}, u32[]{:S(2)}) collective-permute-start(bf16[3,64,1024]{2,1,0:T(8,128)(2,1)} %get-tuple-element.14.refs_0_), channel_id=1, source_target_pairs={{0,1},{1,0},{2,3},{3,2},{4,5},{5,4},{6,7},{7,6},{8,9},{9,8},{10,11... | collective-permute-start | bytes 1179656 | tf_op jit(solution)/shard_map/ppermute | solution.py:183
  13.2 9.3 %collective-permute-start.4 = (bf16[3,64,512]{2,1,0:T(8,128)(2,1)}, bf16[3,64,512]{2,1,0:T(8,128)(2,1)}, u32[]{:S(2)}, u32[]{:S(2)}) collective-permute-start(bf16[3,64,512]{2,1,0:T(8,128)(2,1)} %get-tuple-element.9), channel_id=1, source_target_pairs={{4,0},{6,2},{8,4},{10,6},{12,8},{14,10},{16,12},{18,14},{20,16},{2... | collective-permute-start | bytes 589832 | tf_op jit(solution)/shard_map/ppermute | solution.py:203
  14.5 11.6 %collective-permute-start.5 = (bf16[3,64,512]{2,1,0:T(8,128)(2,1)}, bf16[3,64,512]{2,1,0:T(8,128)(2,1)}, u32[]{:S(2)}, u32[]{:S(2)}) collective-permute-start(bf16[3,64,512]{2,1,0:T(8,128)(2,1)} %get-tuple-element.10), channel_id=1, source_target_pairs={{2,0},{4,2},{6,4},{8,6},{10,8},{12,10},{14,12},{16,14},{18,16},{20... | collective-permute-start | bytes 589832 | tf_op jit(solution)/shard_map/ppermute | solution.py:203
  22.6 41.8 %collective-permute-start.3 = (bf16[3,64,1024]{2,1,0:T(8,128)(2,1)S(1)}, bf16[3,64,1024]{2,1,0:T(8,128)(2,1)}, u32[]{:S(2)}, u32[]{:S(2)}) collective-permute-start(bf16[3,64,1024]{2,1,0:T(8,128)(2,1)S(1)} %get-tuple-element.15.refs_0_), channel_id=1, source_target_pairs={{0,1},{1,0},{2,3},{3,2},{4,5},{5,4},{6,7},{7,6},{8,9},{9,8},{10,11... | collective-permute-start | bytes 1179656 | tf_op jit(solution)/shard_map/ppermute | solution.py:183
  22.6 46.5 %collective-permute-start.2 = (bf16[3,64,1024]{2,1,0:T(8,128)(2,1)S(1)}, bf16[3,64,1024]{2,1,0:T(8,128)(2,1)}, u32[]{:S(2)}, u32[]{:S(2)}) collective-permute-start(bf16[3,64,1024]{2,1,0:T(8,128)(2,1)S(1)} %get-tuple-element.16.refs_0_), channel_id=1, source_target_pairs={{0,1},{1,0},{2,3},{3,2},{4,5},{5,4},{6,7},{7,6},{8,9},{9,8},{10,11... | collective-permute-start | bytes 1179656 | tf_op jit(solution)/shard_map/ppermute | solution.py:183
  26.2 21.2 %collective-permute-start.6 = (bf16[3,64,512]{2,1,0:T(8,128)(2,1)}, bf16[3,64,512]{2,1,0:T(8,128)(2,1)S(1)}, u32[]{:S(2)}, u32[]{:S(2)}) collective-permute-start(bf16[3,64,512]{2,1,0:T(8,128)(2,1)} %get-tuple-element.11), channel_id=1, source_target_pairs={{0,2},{2,4},{4,6},{6,8},{8,10},{10,12},{12,14},{14,16},{16,18},{18... | collective-permute-start | bytes 589832 | tf_op jit(solution)/shard_map/ppermute | solution.py:203
  30.9 17.8 %collective-permute-start.7 = (bf16[3,64,512]{2,1,0:T(8,128)(2,1)}, bf16[3,64,512]{2,1,0:T(8,128)(2,1)S(1)}, u32[]{:S(2)}, u32[]{:S(2)}) collective-permute-start(bf16[3,64,512]{2,1,0:T(8,128)(2,1)} %get-tuple-element.12), channel_id=1, source_target_pairs={{0,4},{2,6},{4,8},{6,10},{8,12},{10,14},{12,16},{14,18},{16,20},{1... | collective-permute-start | bytes 589832 | tf_op jit(solution)/shard_map/ppermute | solution.py:203
  35.0 38.9 %collective-permute-start.1 = (bf16[3,64,1024]{2,1,0:T(8,128)(2,1)S(1)}, bf16[3,64,1024]{2,1,0:T(8,128)(2,1)S(1)}, u32[]{:S(2)}, u32[]{:S(2)}) collective-permute-start(bf16[3,64,1024]{2,1,0:T(8,128)(2,1)S(1)} %get-tuple-element.17.refs_0_), channel_id=1, source_target_pairs={{0,1},{1,0},{2,3},{3,2},{4,5},{5,4},{6,7},{7,6},{8,9},{9,8},{10,11... | collective-permute-start | bytes 1179656 | tf_op jit(solution)/shard_map/ppermute | solution.py:183
  42.8 4.6 %copy-start.4 = (bf16[3,64,512]{2,1,0:T(8,128)(2,1)S(1)}, bf16[3,64,512]{2,1,0:T(8,128)(2,1)}, u32[]{:S(2)}) copy-start(bf16[3,64,512]{2,1,0:T(8,128)(2,1)} %slice.30.refs_0_) | copy-start | bytes 589828
  47.4 2.0 %copy-start.6 = (bf16[3,64,512]{2,1,0:T(8,128)(2,1)}, bf16[3,64,512]{2,1,0:T(8,128)(2,1)S(1)}, u32[]{:S(2)}) copy-start(bf16[3,64,512]{2,1,0:T(8,128)(2,1)S(1)} %collective-permute-done.6.refs_2_) | copy-start | bytes 589828
  47.4 31.9 %collective-permute-start = (bf16[3,64,512]{2,1,0:T(8,128)(2,1)S(1)}, bf16[3,64,512]{2,1,0:T(8,128)(2,1)S(1)}, u32[]{:S(2)}, u32[]{:S(2)}) collective-permute-start(bf16[3,64,512]{2,1,0:T(8,128)(2,1)S(1)} %copy-done.4), channel_id=1, source_target_pairs={{0,1},{1,0},{2,3},{3,2},{4,5},{5,4},{6,7},{7,6},{8,9},{9,8},{10,11... | collective-permute-start | bytes 589832 | tf_op jit(solution)/shard_map/ppermute | solution.py:183
  48.7 0.7 copy-start.7
  73.8 0.8 copy-start.5
  79.3 0.7 copy-start.8
where the time goes:
time: 84.1 us; the launch traced here: 83 us
  Pallas kernels  49.4 us (59%)
  starting transfers between devices  20 us (24%)
  local copies, waits for them, and re-layouts  7.31 us (9%)
  other arithmetic  6.07 us (7%)
    pallas_call x7, Pallas kernels, nonlinear(): call(functools.partial(nonlinear_kernel, shares, adds), (width // tile,),...  29.2 us
    pallas_call x1, Pallas kernels, local(): call(functools.partial(coupling_kernel, per_step, bounds[EARLY] // per_st...  15 us
    ppermute x4, starting transfers between devices, local(): halos.append(lax.ppermute(packed[direction], 'node', pairs))  13.5 us
    ppermute x7, starting transfers between devices, local(): lax.ppermute(piece, 'harm', [(i, (i + by) % shares) for i in range(shares)])  6.54 us
    pallas_call x1, Pallas kernels, local(): call(halo_kernel, (1,), [smem, fixed(points, rows, nodes)], [fixed(points...  3.45 us
    another operation x1, other arithmetic  2.64 us
    slice x2, local copies, waits for them, and re-layouts, local(): piece = x[:, :, low:high].astype(jnp.bfloat16)  1.75 us
    pallas_call x1, Pallas kernels, local(): call(round_kernel, (1,), [fixed(*shape)], fixed(*shape), jax.ShapeDtypeSt...  1.7 us
  transfers between devices with their start and end apart: 11, of which 0 were waited for; matrix products, arithmetic and copies ran while one was open for 14% of the time, Pallas kernels for 54%

commit v1 on v0

--- a/solution.py
+++ b/solution.py
@@ -11,8 +11,8 @@
 LOG_TWO = 0.6931471805599453
 OFFSETS = (-2, -1, 1, 2)
 LANES = 128
-BOUNDS = (0, 4, 12, 20, 28, 36, 44, 48)
-EARLY = 3
+BOUNDS = (0, 8, 24, 40, 48)
+EARLY = 2
 VMEM_BYTES = 60 << 20
 
 
@@ -158,7 +158,7 @@
 
     blocks = nodes // LANES
     bounds = [bound * blocks // BOUNDS[-1] for bound in BOUNDS]
-    unit = 2 if all(bound % 2 == 0 for bound in bounds) else 1
+    unit = 8 if all(bound % 8 == 0 for bound in bounds) else 1
     tile = unit * LANES
     chunk_count = len(bounds) - 1
     own_chunks, arrived = [], []
@@ -243,7 +243,7 @@
         total = nonlinear(chunk, total, False)
 
     count = neighbour_slot.shape[1]
-    per_step = 4 if all(bound % 4 == 0 for bound in bounds) else 1
+    per_step = unit
     step_width = per_step * LANES
     row_ids = me * rows + jnp.arange(rows, dtype=jnp.int32)
     rate = (row_ids // 2).astype(jnp.float32) / (length // 2)

time: 84.1 us -> 72.6 us (0.86)
  the two profiles are of different devices: /device:TPU:1 before, /device:TPU:0 now
where the time goes in v1:
time: 72.6 us; the launch traced here: 72.1 us
  Pallas kernels  36.6 us (50%)
  starting transfers between devices  15.9 us (22%)
  waiting for transfers between devices  8.3 us (11%)
  other arithmetic  6.08 us (8%)
  local copies, waits for them, and re-layouts  5.03 us (7%)
    pallas_call x4, Pallas kernels, nonlinear(): call(functools.partial(nonlinear_kernel, shares, adds), (width // tile,),...  18.9 us
    pallas_call x1, Pallas kernels, local(): call(functools.partial(coupling_kernel, per_step, bounds[EARLY] // per_st...  12.3 us
    ppermute x4, starting transfers between devices, local(): halos.append(lax.ppermute(packed[direction], 'node', pairs))  9.28 us
    ppermute x4, waiting for transfers between devices, local(): lax.ppermute(piece, 'harm', [(i, (i + by) % shares) for i in range(shares)])  8.29 us
    ppermute x4, starting transfers between devices, local(): lax.ppermute(piece, 'harm', [(i, (i + by) % shares) for i in range(shares)])  6.61 us
    pallas_call x1, Pallas kernels, local(): call(halo_kernel, (1,), [smem, fixed(points, rows, nodes)], [fixed(points...  3.44 us
    another operation x1, other arithmetic  2.65 us
    pallas_call x1, Pallas kernels, local(): call(round_kernel, (1,), [fixed(*shape)], fixed(*shape), jax.ShapeDtypeSt...  1.96 us
  transfers between devices with their start and end apart: 8, of which 1 were waited for; matrix products, arithmetic and copies ran while one was open for 9% of the time, Pallas kernels for 45%

profile of v1, /device:TPU:0, one launch (start us, length us, event | category | flops | bytes accessed | tf_op | source)
XLA Modules:
  0.0 72.1 jit_solution(12051713068237322089)
XLA Ops:
  0.0 2.7 %bitcast_convert_fusion = bf16[3,64,6144]{2,1,0:T(8,128)(2,1)S(1)} fusion(f32[64,3,6144]{2,0,1:T(8,128)} %param.12), kind=kLoop, calls=%fused_computation.16 | loop fusion | flops 1179648 | bytes 7077888 | tf_op jit(solution)/shard_map/convert.2
  2.7 1.0 %fusion.1 = (bf16[3,64,2048]{2,1,0:T(8,128)(2,1)}, bf16[3,64,2048]{2,1,0:T(8,128)(2,1)S(1)}) fusion(bf16[3,64,6144]{2,1,0:T(8,128)(2,1)S(1)} %bitcast_convert_fusion), kind=kLoop, calls=%fused_computation.17 | loop fusion | bytes 3145728 | tf_op jit(solution)/shard_map/slice | solution.py:179
  3.7 3.0 %collective-permute-start.6 = (bf16[3,64,2048]{2,1,0:T(8,128)(2,1)}, bf16[3,64,2048]{2,1,0:T(8,128)(2,1)}, u32[]{:S(2)}, u32[]{:S(2)}) collective-permute-start(bf16[3,64,2048]{2,1,0:T(8,128)(2,1)} %get-tuple-element.13.refs_0_), channel_id=1, source_target_pairs={{0,1},{1,0},{2,3},{3,2},{4,5},{5,4},{6,7},{7,6},{8,9},{9,8},{10,11... | collective-permute-start | bytes 2359304 | tf_op jit(solution)/shard_map/ppermute | solution.py:183
  6.6 2.0 %shard_map.119.refs_0_ = bf16[3,64,1024]{2,1,0:T(8,128)(2,1)} custom-call(f32[3,64,6144]{2,1,0:T(8,128)} %bitcast.8), custom_call_target="tpu_custom_call" | custom-call | bytes 1179648 | tf_op jit(solution)/shard_map/pallas_call | solution.py:169
  8.6 0.3 collective-permute-start.7
  8.9 0.2 dynamic-slice_reduce_fusion
  9.1 0.7 reshape_squeeze.3.list_ref
  9.8 3.4 %shard_map.118 = (bf16[3,64,512]{2,1,0:T(8,128)(2,1)}, bf16[3,64,512]{2,1,0:T(8,128)(2,1)}, bf16[3,64,512]{2,1,0:T(8,128)(2,1)}, bf16[3,64,512]{2,1,0:T(8,128)(2,1)}) custom-call(s32[16]{0:T(128)} %reshape_squeeze.3.list_ref, f32[3,64,6144]{2,1,0:T(8,128)} %bitcast.9), custom_call_target="tpu_custom_call" | custom-call | bytes 4718592 | tf_op jit(solution)/shard_map/pallas_call | solution.py:190
  13.2 1.3 %collective-permute-start.2 = (bf16[3,64,512]{2,1,0:T(8,128)(2,1)}, bf16[3,64,512]{2,1,0:T(8,128)(2,1)}, u32[]{:S(2)}, u32[]{:S(2)}) collective-permute-start(bf16[3,64,512]{2,1,0:T(8,128)(2,1)} %get-tuple-element.9), channel_id=1, source_target_pairs={{4,0},{6,2},{8,4},{10,6},{12,8},{14,10},{16,12},{18,14},{20,16},{2... | collective-permute-start | bytes 589832 | tf_op jit(solution)/shard_map/ppermute | solution.py:203
  14.5 1.3 %collective-permute-start.3 = (bf16[3,64,512]{2,1,0:T(8,128)(2,1)}, bf16[3,64,512]{2,1,0:T(8,128)(2,1)}, u32[]{:S(2)}, u32[]{:S(2)}) collective-permute-start(bf16[3,64,512]{2,1,0:T(8,128)(2,1)} %get-tuple-element.10), channel_id=1, source_target_pairs={{2,0},{4,2},{6,4},{8,6},{10,8},{12,10},{14,12},{16,14},{18,16},{20... | collective-permute-start | bytes 589832 | tf_op jit(solution)/shard_map/ppermute | solution.py:203
  15.8 1.8 %collective-permute-start.1 = (bf16[3,64,2048]{2,1,0:T(8,128)(2,1)S(1)}, bf16[3,64,2048]{2,1,0:T(8,128)(2,1)}, u32[]{:S(2)}, u32[]{:S(2)}) collective-permute-start(bf16[3,64,2048]{2,1,0:T(8,128)(2,1)S(1)} %get-tuple-element.14.refs_0_), channel_id=1, source_target_pairs={{0,1},{1,0},{2,3},{3,2},{4,5},{5,4},{6,7},{7,6},{8,9},{9,8},{10,11... | collective-permute-start | bytes 2359304 | tf_op jit(solution)/shard_map/ppermute | solution.py:183
  17.6 0.1 constant_dynamic-slice_fusion.1
  17.7 0.7 fusion
  18.4 0.7 subtract_convert_fusion
  19.2 0.1 copy.17
  19.3 0.7 reshape.53.slot_ref
  19.9 0.7 %dynamic-slice_convert_fusion = (bf16[64,128]{1,0:T(8,128)(2,1)S(1)}, bf16[64,128]{1,0:T(8,128)(2,1)S(1)}) fusion(bf16[128,128]{1,0:T(8,128)(2,1)} %constant.82, s32[]{:T(128)S(6)} %select_n.55, bf16[128,128]{1,0:T(8,128)(2,1)} %constant.83), kind=kLoop, calls=%fused_computation.4 | loop fusion | bytes 65540 | tf_op jit(solution)/shard_map/convert.4
  20.7 0.6 pad_maximum_fusion.2.analysis_ref
  21.3 1.4 %pad_maximum_fusion.1.synthesis_ref = bf16[128,256]{1,0:T(8,128)(2,1)} fusion(bf16[128,128]{1,0:T(8,128)(2,1)} %subtract_convert_fusion, bf16[128,128]{1,0:T(8,128)(2,1)} %fusion), kind=kLoop, calls=%fused_computation.1 | loop fusion | flops 131072 | bytes 131072 | tf_op jit(solution)/shard_map/concatenate | solution.py:212
  22.7 2.8 %collective-permute-start.4 = (bf16[3,64,512]{2,1,0:T(8,128)(2,1)}, bf16[3,64,512]{2,1,0:T(8,128)(2,1)S(1)}, u32[]{:S(2)}, u32[]{:S(2)}) collective-permute-start(bf16[3,64,512]{2,1,0:T(8,128)(2,1)} %get-tuple-element.11), channel_id=1, source_target_pairs={{0,2},{2,4},{4,6},{6,8},{8,10},{10,12},{12,14},{14,16},{16,18},{18... | collective-permute-start | bytes 589832 | tf_op jit(solution)/shard_map/ppermute | solution.py:203
  25.5 8.3 %collective-permute-done.7.refs_1_ = bf16[3,64,1024]{2,1,0:T(8,128)(2,1)} collective-permute-done((bf16[3,64,1024]{2,1,0:T(8,128)(2,1)}, bf16[3,64,1024]{2,1,0:T(8,128)(2,1)}, u32[]{:S(2)}, u32[]{:S(2)}) %collective-permute-start.7) | collective-permute-done | bytes 393248 | tf_op jit(solution)/shard_map/ppermute | solution.py:183
  33.8 4.0 %collective-permute-start.5 = (bf16[3,64,512]{2,1,0:T(8,128)(2,1)}, bf16[3,64,512]{2,1,0:T(8,128)(2,1)S(1)}, u32[]{:S(2)}, u32[]{:S(2)}) collective-permute-start(bf16[3,64,512]{2,1,0:T(8,128)(2,1)} %get-tuple-element.12), channel_id=1, source_target_pairs={{0,4},{2,6},{4,8},{6,10},{8,12},{10,14},{12,16},{14,18},{16,20},{1... | collective-permute-start | bytes 589832 | tf_op jit(solution)/shard_map/ppermute | solution.py:203
  37.7 1.6 %collective-permute-start = (bf16[3,64,1024]{2,1,0:T(8,128)(2,1)S(1)}, bf16[3,64,1024]{2,1,0:T(8,128)(2,1)S(1)}, u32[]{:S(2)}, u32[]{:S(2)}) collective-permute-start(bf16[3,64,1024]{2,1,0:T(8,128)(2,1)S(1)} %slice.15.refs_0_), channel_id=1, source_target_pairs={{0,1},{1,0},{2,3},{3,2},{4,5},{5,4},{6,7},{7,6},{8,9},{9,8},{10,11... | collective-permute-start | bytes 1179656 | tf_op jit(solution)/shard_map/ppermute | solution.py:183
  39.3 3.7 %shard_map.120.refs_5_ = f32[3,64,6144]{2,1,0:T(8,128)} custom-call(bf16[128,256]{1,0:T(8,128)(2,1)} %pad_maximum_fusion.1.synthesis_ref, bf16[64,256]{1,0:T(8,128)(2,1)} %pad_maximum_fusion.2.analysis_ref, bf16[3,64,1024]{2,1,0:T(8,128)(2,1)} %shard_map.119.refs_0_, bf16[3,64,1024]{2,1,0:T(8,128)(2,1)} %collective-permute-done.7.refs_1_, ...), custom_call_target="tpu_custom_call" | custom-call | flops 402653184 | bytes 2359296 | tf_op jit(solution)/shard_map/pallas_call | solution.py:227
  43.0 5.5 %shard_map.121.refs_8_ = f32[3,64,6144]{2,1,0:T(8,128)} custom-call(bf16[128,256]{1,0:T(8,128)(2,1)} %pad_maximum_fusion.1.synthesis_ref, bf16[64,256]{1,0:T(8,128)(2,1)} %pad_maximum_fusion.2.analysis_ref, bf16[3,64,2048]{2,1,0:T(8,128)(2,1)} %get-tuple-element.13.refs_0_, ...), custom_call_target="tpu_custom_call", output_to_operand_aliasing={{}: (7, {})} | custom-call | flops 805306368 | bytes 4718592 | tf_op jit(solution)/shard_map/pallas_call | solution.py:227
  48.5 0.0 collective-permute-done.3.refs_1_
  48.5 0.0 collective-permute-done.5.refs_3_
  48.5 0.7 %broadcast_in_dim.2.refs_7_ = f32[64,128]{1,0:T(8,128)} broadcast(f32[64]{0:T(128)S(1)} %compare_select_fusion), dimensions={0} | broadcast | bytes 33024 | tf_op jit(solution)/shard_map/broadcast_in_dim | solution.py:251
  49.3 12.3 %shard_map.122.refs_5_ = f32[3,64,6144]{2,1,0:T(8,128)} custom-call(s32[192]{0:T(256)} %reshape.53.slot_ref, f32[3,64,6144]{2,1,0:T(8,128)} %bitcast.10, bf16[3,64,512]{2,1,0:T(8,128)(2,1)} %collective-permute-done.2.refs_0_, bf16[3,64,512]{2,1,0:T(8,128)(2,1)} %collective-permute-done.3.refs_1_, ...), custom_call_target="tpu_custom_call", output_to_operand_aliasing={{}: (10, {})} | custom-call | flops 1207959552 | bytes 20447232 | tf_op jit(solution)/shard_map/pallas_call | solution.py:253
  61.6 5.8 %shard_map.123.refs_5_ = f32[3,64,6144]{2,1,0:T(8,128)} custom-call(bf16[128,256]{1,0:T(8,128)(2,1)} %pad_maximum_fusion.1.synthesis_ref, bf16[64,256]{1,0:T(8,128)(2,1)} %pad_maximum_fusion.2.analysis_ref, bf16[3,64,2048]{2,1,0:T(8,128)(2,1)} %copy-done.1, bf16[3,64,2048]{2,1,0:T(8,128)(2,1)} %collective-permute-done.1.refs_1_, ...), custom_call_target="tpu_custom_call", output_to_operand_aliasing={{}: (7, {})} | custom-call | flops 805306368 | bytes 4718592 | tf_op jit(solution)/shard_map/pallas_call | solution.py:227
  67.3 0.7 %copy-done.3 = bf16[3,64,1024]{2,1,0:T(8,128)(2,1)} copy-done((bf16[3,64,1024]{2,1,0:T(8,128)(2,1)}, bf16[3,64,1024]{2,1,0:T(8,128)(2,1)S(1)}, u32[]{:S(2)}) %copy-start.3) | copy-done | bytes 393240
  68.1 4.0 %shard_map.124 = f32[3,64,6144]{2,1,0:T(8,128)} custom-call(bf16[128,256]{1,0:T(8,128)(2,1)} %pad_maximum_fusion.1.synthesis_ref, bf16[64,256]{1,0:T(8,128)(2,1)} %pad_maximum_fusion.2.analysis_ref, bf16[3,64,1024]{2,1,0:T(8,128)(2,1)} %copy-done.2, bf16[3,64,1024]{2,1,0:T(8,128)(2,1)} %copy-done.3, ...), custom_call_target="tpu_custom_call", output_to_operand_aliasing={{}: (7, {})} | custom-call | flops 402653184 | bytes 2359296 | tf_op jit(solution)/shard_map/pallas_call | solution.py:227
  (22 shorter events, 0.1 us)
Async XLA Ops:
  0.0 8.9 %copy-start = (s32[16,4,4]{0,2,1:T(4,128)S(1)}, s32[16,4,4]{0,2,1:T(4,128)}, u32[]{:S(2)}) copy-start(s32[16,4,4]{0,2,1:T(4,128)} %param.19) | copy-start | bytes 3076
  3.7 12.1 %copy-start.1 = (bf16[3,64,2048]{2,1,0:T(8,128)(2,1)}, bf16[3,64,2048]{2,1,0:T(8,128)(2,1)S(1)}, u32[]{:S(2)}) copy-start(bf16[3,64,2048]{2,1,0:T(8,128)(2,1)S(1)} %get-tuple-element.14.refs_0_) | copy-start | bytes 2359300
  3.7 34.1 %collective-permute-start.6 = (bf16[3,64,2048]{2,1,0:T(8,128)(2,1)}, bf16[3,64,2048]{2,1,0:T(8,128)(2,1)}, u32[]{:S(2)}, u32[]{:S(2)}) collective-permute-start(bf16[3,64,2048]{2,1,0:T(8,128)(2,1)} %get-tuple-element.13.refs_0_), channel_id=1, source_target_pairs={{0,1},{1,0},{2,3},{3,2},{4,5},{5,4},{6,7},{7,6},{8,9},{9,8},{10,11... | collective-permute-start | bytes 2359304 | tf_op jit(solution)/shard_map/ppermute | solution.py:183
  6.6 11.0 %copy-start.4 = (f32[128,128]{1,0:T(8,128)S(1)}, f32[128,128]{1,0:T(8,128)}, u32[]{:S(2)}) copy-start(f32[128,128]{1,0:T(8,128)} %constant.63.clone) | copy-start | bytes 196612
  6.6 12.5 %copy-start.7 = (s32[48,4]{0,1:T(4,128)S(1)}, s32[48,4]{0,1:T(4,128)}, u32[]{:S(2)}) copy-start(s32[48,4]{0,1:T(4,128)} %param.20) | copy-start | bytes 2308
  8.6 25.2 %collective-permute-start.7 = (bf16[3,64,1024]{2,1,0:T(8,128)(2,1)}, bf16[3,64,1024]{2,1,0:T(8,128)(2,1)}, u32[]{:S(2)}, u32[]{:S(2)}) collective-permute-start(bf16[3,64,1024]{2,1,0:T(8,128)(2,1)} %shard_map.119.refs_0_), channel_id=1, source_target_pairs={{0,1},{1,0},{2,3},{3,2},{4,5},{5,4},{6,7},{7,6},{8,9},{9,8},{10,11... | collective-permute-start | bytes 1179656 | tf_op jit(solution)/shard_map/ppermute | solution.py:183
  13.2 9.5 %collective-permute-start.2 = (bf16[3,64,512]{2,1,0:T(8,128)(2,1)}, bf16[3,64,512]{2,1,0:T(8,128)(2,1)}, u32[]{:S(2)}, u32[]{:S(2)}) collective-permute-start(bf16[3,64,512]{2,1,0:T(8,128)(2,1)} %get-tuple-element.9), channel_id=1, source_target_pairs={{4,0},{6,2},{8,4},{10,6},{12,8},{14,10},{16,12},{18,14},{20,16},{2... | collective-permute-start | bytes 589832 | tf_op jit(solution)/shard_map/ppermute | solution.py:203
  14.5 34.0 %collective-permute-start.3 = (bf16[3,64,512]{2,1,0:T(8,128)(2,1)}, bf16[3,64,512]{2,1,0:T(8,128)(2,1)}, u32[]{:S(2)}, u32[]{:S(2)}) collective-permute-start(bf16[3,64,512]{2,1,0:T(8,128)(2,1)} %get-tuple-element.10), channel_id=1, source_target_pairs={{2,0},{4,2},{6,4},{8,6},{10,8},{12,10},{14,12},{16,14},{18,16},{20... | collective-permute-start | bytes 589832 | tf_op jit(solution)/shard_map/ppermute | solution.py:203
  15.8 45.8 %collective-permute-start.1 = (bf16[3,64,2048]{2,1,0:T(8,128)(2,1)S(1)}, bf16[3,64,2048]{2,1,0:T(8,128)(2,1)}, u32[]{:S(2)}, u32[]{:S(2)}) collective-permute-start(bf16[3,64,2048]{2,1,0:T(8,128)(2,1)S(1)} %get-tuple-element.14.refs_0_), channel_id=1, source_target_pairs={{0,1},{1,0},{2,3},{3,2},{4,5},{5,4},{6,7},{7,6},{8,9},{9,8},{10,11... | collective-permute-start | bytes 2359304 | tf_op jit(solution)/shard_map/ppermute | solution.py:183
  19.2 29.3 %copy-start.2 = (bf16[3,64,1024]{2,1,0:T(8,128)(2,1)}, bf16[3,64,1024]{2,1,0:T(8,128)(2,1)S(1)}, u32[]{:S(2)}) copy-start(bf16[3,64,1024]{2,1,0:T(8,128)(2,1)S(1)} %slice.15.refs_0_) | copy-start | bytes 1179652
  22.7 25.8 %collective-permute-start.4 = (bf16[3,64,512]{2,1,0:T(8,128)(2,1)}, bf16[3,64,512]{2,1,0:T(8,128)(2,1)S(1)}, u32[]{:S(2)}, u32[]{:S(2)}) collective-permute-start(bf16[3,64,512]{2,1,0:T(8,128)(2,1)} %get-tuple-element.11), channel_id=1, source_target_pairs={{0,2},{2,4},{4,6},{6,8},{8,10},{10,12},{12,14},{14,16},{16,18},{18... | collective-permute-start | bytes 589832 | tf_op jit(solution)/shard_map/ppermute | solution.py:203
  33.8 14.8 %collective-permute-start.5 = (bf16[3,64,512]{2,1,0:T(8,128)(2,1)}, bf16[3,64,512]{2,1,0:T(8,128)(2,1)S(1)}, u32[]{:S(2)}, u32[]{:S(2)}) collective-permute-start(bf16[3,64,512]{2,1,0:T(8,128)(2,1)} %get-tuple-element.12), channel_id=1, source_target_pairs={{0,4},{2,6},{4,8},{6,10},{8,12},{10,14},{12,16},{14,18},{16,20},{1... | collective-permute-start | bytes 589832 | tf_op jit(solution)/shard_map/ppermute | solution.py:203
  37.7 29.6 %collective-permute-start = (bf16[3,64,1024]{2,1,0:T(8,128)(2,1)S(1)}, bf16[3,64,1024]{2,1,0:T(8,128)(2,1)S(1)}, u32[]{:S(2)}, u32[]{:S(2)}) collective-permute-start(bf16[3,64,1024]{2,1,0:T(8,128)(2,1)S(1)} %slice.15.refs_0_), channel_id=1, source_target_pairs={{0,1},{1,0},{2,3},{3,2},{4,5},{5,4},{6,7},{7,6},{8,9},{9,8},{10,11... | collective-permute-start | bytes 1179656 | tf_op jit(solution)/shard_map/ppermute | solution.py:183
  48.5 0.8 %copy-start.5 = (bf16[3,64,512]{2,1,0:T(8,128)(2,1)}, bf16[3,64,512]{2,1,0:T(8,128)(2,1)S(1)}, u32[]{:S(2)}) copy-start(bf16[3,64,512]{2,1,0:T(8,128)(2,1)S(1)} %collective-permute-done.4.refs_2_) | copy-start | bytes 589828
  48.5 0.7 %copy-start.6 = (bf16[3,64,512]{2,1,0:T(8,128)(2,1)}, bf16[3,64,512]{2,1,0:T(8,128)(2,1)S(1)}, u32[]{:S(2)}) copy-start(bf16[3,64,512]{2,1,0:T(8,128)(2,1)S(1)} %collective-permute-done.5.refs_3_) | copy-start | bytes 589828
  67.3 0.8 %copy-start.3 = (bf16[3,64,1024]{2,1,0:T(8,128)(2,1)}, bf16[3,64,1024]{2,1,0:T(8,128)(2,1)S(1)}, u32[]{:S(2)}) copy-start(bf16[3,64,1024]{2,1,0:T(8,128)(2,1)S(1)} %collective-permute-done.refs_1_) | copy-start | bytes 1179652
